TPU v7x, 32 devices: a whole 2x2x4 slice. The times are simulated.
32 devices in a mesh: row: 8 (over z, y), col: 4 (over x, core).
Axes of the slice: x: 2, y: 2, z: 4, core: 2. Of those that a mesh axis runs over, the one named last changes fastest.
Arguments:
- tile_values: bfloat16 [128, 8, 256, 256], P(('row', 'col')), may hold values from -0.375 to 0.375
- block_columns: int32 [128, 8], P(('row', 'col')), may hold values from 0 to 127, as said below
- tile_counts: int32 [128], P(('row', 'col')), may hold values from 1 to 8, as said below
- diagonal: float32 [32768], P(('row', 'col')), may hold values from 0.5 to 4
- sketch_rows: int32 [32768], P(('row', 'col')), may hold values from 0 to 1023
- sketch_signs: int32 [32768], P(('row', 'col')), may hold values from 0 to 1
- right_side: float32 [16, 32768], P(None, ('row', 'col')), may hold values from -70 to 70
Outputs:
- solution: float32 [16, 32768], P(None, ('row', 'col'))
- last_basis: float32 [16, 32768], P(None, ('row', 'col'))
- hessenberg: float32 [16, 5, 4], replicated
Inputs may be any that keep to these rules, and one draw needn't show every extreme that they name: `block_columns`: for block row b all 8 entries are distinct block columns c with (c - b) mod 128 <= 4 or >= 124; only slots k < tile_counts[b] are used. `tile_counts`: in every draw the 4 block rows of at least one device all have 8.
All inputs are finite; a program needn't handle non-finite values.
Results may differ from a plain program's by a relative error of at most 0.0053.
Values may be sent and summed in bfloat16 or wider, within the bound.
A program may use at most 64 MiB of HBM per device.

v0:
```python
import math
import jax
import jax.numpy as jnp
from jax import lax
from jax.sharding import PartitionSpec as P

SKETCH = 1024
ITERS = 4
epsilon = 1e-06
highest = lax.Precision.HIGHEST


def with_halo(block, sides, width):
    for axis, dim in sides:
        count = lax.axis_size(axis)
        forward = [(i, i + 1) for i in range(count - 1)]
        forward.append((count - 1, 0))
        backward = [(target, source) for source, target in forward]
        low = lax.ppermute(
            lax.slice_in_dim(block, block.shape[dim] - width, None, axis=dim), axis, forward
        )
        high = lax.ppermute(lax.slice_in_dim(block, 0, width, axis=dim), axis, backward)
        block = jnp.concatenate([low, block, high], axis=dim)
    return block


def cholesky_solve(gram, target):
    order = gram.shape[1]
    factor = {}
    for column in range(order):
        diag_part = gram[:, column, column]
        for inner in range(column):
            diag_part = diag_part - factor[column, inner] * factor[column, inner]
        factor[column, column] = jnp.sqrt(diag_part)
        for below in range(column + 1, order):
            entry = gram[:, below, column]
            for inner in range(column):
                entry = entry - factor[below, inner] * factor[column, inner]
            factor[below, column] = entry / factor[column, column]
    forward = []
    for column in range(order):
        entry = target[:, column]
        for inner in range(column):
            entry = entry - factor[column, inner] * forward[inner]
        forward.append(entry / factor[column, column])
    result = [None] * order
    for column in reversed(range(order)):
        entry = forward[column]
        for inner in range(column + 1, order):
            entry = entry - factor[inner, column] * result[inner]
        result[column] = entry / factor[column, column]
    return jnp.stack(result, axis=1)


def sketch_solve(stacked, image_sketch):
    gram = jnp.einsum("rjk,rmk->rjm", stacked, stacked, precision=highest)
    target = jnp.einsum("rjk,rk->rj", stacked, image_sketch, precision=highest)
    return cholesky_solve(gram, target)


def local(tile_values, block_columns, tile_counts, diagonal, sketch_rows, sketch_signs, right_side):
    col_count = lax.axis_size("col")
    devices = lax.axis_size("row") * col_count
    device_index = lax.axis_index("row") * col_count + lax.axis_index("col")
    block_rows = tile_values.shape[0]
    slot_count = tile_values.shape[1]
    tile_size = tile_values.shape[2]
    systems = right_side.shape[0]
    all_blocks = block_rows * devices
    scaling = 1.0 / math.sqrt(all_blocks * tile_size)
    signed = (2 * sketch_signs - 1).astype(jnp.float32) * scaling
    projector = jnp.where(sketch_rows[:, None] == jnp.arange(SKETCH)[None, :], signed[:, None], 0.0)
    live_mask = jnp.arange(slot_count)[None, :] < tile_counts[:, None]
    first_block = device_index * block_rows
    turns = jnp.max(jnp.sum(live_mask.astype(jnp.int32), axis=1))
    live_weight = live_mask.astype(jnp.float32)
    start = lax.psum(jnp.dot(right_side, projector, precision=highest), ("row", "col"))
    beta = jnp.sqrt(jnp.sum(start * start, axis=1) + epsilon)
    basis = [right_side / beta[:, None]]
    sketched = [start / beta[:, None]]
    columns_list = []
    for step_index in range(ITERS):
        vector = basis[-1]
        shadow = vector.astype(jnp.bfloat16)
        widened = with_halo(shadow, ((("row", "col"), 1),), block_rows * tile_size)
        start_block = first_block - block_rows
        blocks = widened.reshape(systems, widened.shape[1] // tile_size, tile_size)
        local_index = (block_columns - start_block) % all_blocks

        def add_slot(slot_turn, running):
            slot_tiles = lax.dynamic_index_in_dim(tile_values, slot_turn, 1, keepdims=False)
            wanted = lax.dynamic_index_in_dim(local_index, slot_turn, 1, keepdims=False)
            picked = jnp.take(blocks, wanted, axis=1)
            weight_mask = lax.dynamic_index_in_dim(live_weight, slot_turn, 1, keepdims=False)
            product = jnp.einsum(
                "rbi,boi->rbo", picked, slot_tiles, preferred_element_type=jnp.float32
            )
            return running + product * weight_mask[None, :, None]

        tile_sum = lax.fori_loop(
            0, turns, add_slot, jnp.zeros((systems, block_rows, tile_size), jnp.float32)
        )
        image = diagonal[None, :] * vector + tile_sum.reshape(systems, block_rows * tile_size)
        image_sketch = lax.psum(jnp.dot(image, projector, precision=highest), ("row", "col"))
        stacked = jnp.stack(sketched, axis=1)
        coeffs = sketch_solve(stacked, image_sketch)
        fresh = image - jnp.einsum(
            "rj,rjn->rn", coeffs, jnp.stack(basis, axis=1), precision=highest
        )
        fresh_sketch = image_sketch - jnp.einsum("rj,rjk->rk", coeffs, stacked, precision=highest)
        norm_new = jnp.sqrt(jnp.sum(fresh_sketch * fresh_sketch, axis=1) + epsilon)
        basis.append(fresh / norm_new[:, None])
        sketched.append(fresh_sketch / norm_new[:, None])
        padding = jnp.zeros((systems, ITERS - step_index - 1), jnp.float32)
        columns_list.append(jnp.concatenate([coeffs, norm_new[:, None], padding], axis=1))
    hessenberg = jnp.stack(columns_list, axis=2)
    gram = jnp.einsum("rim,rin->rmn", hessenberg, hessenberg, precision=highest)
    weights = cholesky_solve(gram, beta[:, None] * hessenberg[:, 0, :])
    solution = jnp.einsum(
        "rm,rmn->rn", weights, jnp.stack(basis[:ITERS], axis=1), precision=highest
    )
    return (solution, basis[-1], hessenberg)


def solution(mesh):
    in_specs = (
        P(("row", "col"), None, None, None),
        P(("row", "col"), None),
        P(("row", "col")),
        P(("row", "col")),
        P(("row", "col")),
        P(("row", "col")),
        P(None, ("row", "col")),
    )
    out_specs = (P(None, ("row", "col")), P(None, ("row", "col")), P())
    return jax.shard_map(local, mesh=mesh, in_specs=in_specs, out_specs=out_specs, check_vma=False)
```

profile of v0, /device:TPU:1, one launch (start us, length us, event | category | flops | bytes accessed | tf_op | source)
XLA Modules:
  0.0 768.0 jit_solution(5249777427383235755)
XLA Ops:
  7.9 4.2 fusion.73
  13.6 123.9 %all-reduce.6.cloned.1.call-done = f32[16,1024]{1,0:T(8,128)} async-done(((f32[16,1024]{1,0:T(8,128)}), f32[16,1024]{1,0:T(8,128)}) %all-reduce.6.cloned.1.call-update) | async-done | bytes 65552 | tf_op jit(solution)/shard_map/psum | solution.py:77
  139.5 1.7 collective-permute-start
  141.9 4.5 copy.86
  147.1 8.4 %while.40 = (s32[]{:T(128)}, f32[16,4,256]{2,0,1:T(8,128)S(1)}, s32[]{:T(128)}, bf16[4,8,256,256]{3,2,0,1:T(8,128)(2,1)}, s32[4,8]{0,1:T(8,128)S(1)}, /*index=5*...) while((s32[]{:T(128)}, f32[16,4,256]{2,0,1:T(8,128)S(1)}, ...), condition=%wide.region_5.7_spmd, body=%wide.region_4.6_spmd.sunk | while | flops 8438813 | bytes 758035 | solution.py:100
  155.6 3.2 fusion.54
  159.0 131.3 %all-reduce.8.cloned.1.call-done = f32[16,1024]{1,0:T(8,128)} async-done(((f32[16,1024]{1,0:T(8,128)}), f32[16,1024]{1,0:T(8,128)}) %all-reduce.8.cloned.1.call-update) | async-done | bytes 65552 | tf_op jit(solution)/shard_map/psum | solution.py:104
  293.5 1.7 collective-permute-start.2
  296.8 1.6 collective-permute-done.2
  298.4 8.4 %while.41 = (s32[]{:T(128)}, f32[16,4,256]{2,0,1:T(8,128)S(1)}, s32[]{:T(128)}, bf16[4,8,256,256]{3,2,0,1:T(8,128)(2,1)}, s32[4,8]{0,1:T(8,128)S(1)}, /*index=5*...) while((s32[]{:T(128)}, f32[16,4,256]{2,0,1:T(8,128)S(1)}, ...), condition=%wide.region_9.11_spmd, body=%wide.region_8.10_spmd.sunk | while | flops 8438813 | bytes 758035 | solution.py:100
  306.8 3.1 fusion.52
  310.3 132.5 %all-reduce.10.cloned.1.call-done = f32[16,1024]{1,0:T(8,128)} async-done(((f32[16,1024]{1,0:T(8,128)}), f32[16,1024]{1,0:T(8,128)}) %all-reduce.10.cloned.1.call-update) | async-done | bytes 65552 | tf_op jit(solution)/shard_map/psum | solution.py:104
  442.8 2.0 fusion.98
  448.3 1.7 collective-permute-start.4
  451.6 1.5 collective-permute-done.4
  453.2 8.4 %while.42 = (s32[]{:T(128)}, f32[16,4,256]{2,0,1:T(8,128)S(1)}, s32[]{:T(128)}, bf16[4,8,256,256]{3,2,0,1:T(8,128)(2,1)}, s32[4,8]{0,1:T(8,128)S(1)}, /*index=5*...) while((s32[]{:T(128)}, f32[16,4,256]{2,0,1:T(8,128)S(1)}, ...), condition=%wide.region_13.15_spmd, body=%wide.region_12.14_spmd.sunk | while | flops 8438813 | bytes 758035 | solution.py:100
  461.6 3.1 fusion.50
  465.0 132.7 %all-reduce.12.cloned.1.call-done = f32[16,1024]{1,0:T(8,128)} async-done(((f32[16,1024]{1,0:T(8,128)}), f32[16,1024]{1,0:T(8,128)}) %all-reduce.12.cloned.1.call-update) | async-done | bytes 65552 | tf_op jit(solution)/shard_map/psum | solution.py:104
  597.6 2.0 fusion.78
  603.2 1.7 collective-permute-start.6
  608.1 8.6 %while.43 = (s32[]{:T(128)}, f32[16,4,256]{2,0,1:T(8,128)S(1)}, s32[]{:T(128)}, bf16[4,8,256,256]{3,2,0,1:T(8,128)(2,1)}, s32[4,8]{0,1:T(8,128)S(1)}, /*index=5*...) while((s32[]{:T(128)}, f32[16,4,256]{2,0,1:T(8,128)S(1)}, ...), condition=%wide.region_17.19_spmd, body=%wide.region_16.18_spmd.sunk | while | flops 8438813 | bytes 758035 | solution.py:100
  616.8 3.1 fusion.48
  620.1 132.7 %all-reduce.14.cloned.1.call-done = f32[16,1024]{1,0:T(8,128)} async-done(((f32[16,1024]{1,0:T(8,128)}), f32[16,1024]{1,0:T(8,128)}) %all-reduce.14.cloned.1.call-update) | async-done | bytes 65552 | tf_op jit(solution)/shard_map/psum | solution.py:104
  752.8 2.1 fusion.90
  (183 shorter events, 52.0 us)
Async XLA Ops:
  7.2 130.4 %all-reduce.6.cloned.1.call-start = ((), (), s32[]{:S(2)}) async-start(), calls=%async_computation | async-start | bytes 131072 | tf_op jit(solution)/shard_map/psum | solution.py:77
  12.1 278.2 %all-reduce.8.cloned.1.call-start = ((), (), s32[]{:S(2)}) async-start(), calls=%async_computation.1 | async-start | bytes 131072 | tf_op jit(solution)/shard_map/psum | solution.py:104
  139.4 7.7 collective-permute-start.1
  139.5 7.6 collective-permute-start
  146.4 9.1 %copy-start.1 = (f32[16,1024]{1,0:T(8,128)S(1)}, f32[16,1024]{1,0:T(8,128)}, u32[]{:S(2)}) copy-start(f32[16,1024]{1,0:T(8,128)} %param.23) | copy-start | bytes 196612
  146.4 9.1 %copy-start.2 = (f32[1024]{0:T(1024)S(1)}, f32[1024]{0:T(1024)}, u32[]{:S(2)}) copy-start(f32[1024]{0:T(1024)} %param.20) | copy-start | bytes 12292
  146.4 9.1 %copy-start.3 = (s32[1024]{0:T(1024)S(1)}, s32[1024]{0:T(1024)}, u32[]{:S(2)}) copy-start(s32[1024]{0:T(1024)} %param.21) | copy-start | bytes 12292
  146.4 143.9 %copy-start = (f32[16,1024]{1,0:T(8,128)S(1)}, f32[16,1024]{1,0:T(8,128)}, u32[]{:S(2)}) copy-start(f32[16,1024]{1,0:T(8,128)} %all-reduce.6.cloned.1.call-done) | copy-start | bytes 196612
  158.8 284.1 %all-reduce.10.cloned.1.call-start = ((), (), s32[]{:S(2)}) async-start(), calls=%async_computation.2 | async-start | bytes 131072 | tf_op jit(solution)/shard_map/psum | solution.py:104
  293.4 3.4 collective-permute-start.3
  293.5 4.9 collective-permute-start.2
  310.0 287.6 %all-reduce.12.cloned.1.call-start = ((), (), s32[]{:S(2)}) async-start(), calls=%async_computation.3 | async-start | bytes 131072 | tf_op jit(solution)/shard_map/psum | solution.py:104
  448.2 3.4 collective-permute-start.5
  448.3 4.9 collective-permute-start.4
  464.8 288.0 %all-reduce.14.cloned.1.call-start = ((), (), s32[]{:S(2)}) async-start(), calls=%async_computation.4 | async-start | bytes 131072 | tf_op jit(solution)/shard_map/psum | solution.py:104
  603.1 3.5 collective-permute-start.7
  603.2 4.9 collective-permute-start.6
Sparse Core Ops, SparseCore 0:
  14.1 123.3 all-reduce.5
  158.9 131.3 all-reduce.7
  310.1 132.6 all-reduce.9
  464.9 132.6 all-reduce.11
  620.1 132.6 all-reduce.13
where the time goes:
time: 771 us; the launch traced here: 768 us
  waiting for transfers between devices  658 us (85%)
  matrix products  46.8 us (6%)
  local copies, waits for them, and re-layouts  16.1 us (2%)
  other arithmetic  14.3 us (2%)
  between operations  14.2 us (2%)
  loops' own time  11.2 us (1%)
    psum x4, waiting for transfers between devices, local(): lax.psum(jnp.dot(image, projector, precision=highest), ('row', 'col'))  529 us
    psum x1, waiting for transfers between devices, local(): lax.psum(jnp.dot(right_side, projector, precision=highest), ('row', 'col'))  124 us
    dot_general x12, matrix products, add_slot(): jnp.einsum('rbi,boi->rbo', picked, slot_tiles, preferred_element_type=jnp...  15.7 us
  transfers between devices with their start and end apart: 13, of which 9 were waited for; matrix products, arithmetic and copies ran while one was open for 2% of the time, Pallas kernels for 0%

commit v1 on v0

--- a/solution.py
+++ b/solution.py
@@ -74,7 +74,9 @@
     first_block = device_index * block_rows
     turns = jnp.max(jnp.sum(live_mask.astype(jnp.int32), axis=1))
     live_weight = live_mask.astype(jnp.float32)
-    start = lax.psum(jnp.dot(right_side, projector, precision=highest), ("row", "col"))
+    start = jnp.sum(
+        lax.all_gather(jnp.dot(right_side, projector, precision=highest), ("row", "col")), axis=0
+    )
     beta = jnp.sqrt(jnp.sum(start * start, axis=1) + epsilon)
     basis = [right_side / beta[:, None]]
     sketched = [start / beta[:, None]]

time: 771 us -> 704 us (0.913)
  waiting for transfers between devices: 658 us -> 592 us
    psum x1 -> x0, waiting for transfers between devices: 124 us -> none  [local(): lax.psum(jnp.dot(right_side, projector, precision=highest), ('row', 'col'))]
    all_gather x0 -> x1, waiting for transfers between devices: none -> 57.3 us  [local(): lax.all_gather(jnp.dot(right_side, projector, precision=highest), ('row',...]
where the time goes in v1:
time: 704 us; the launch traced here: 701 us
  waiting for transfers between devices  592 us (84%)
  matrix products  46.8 us (7%)
  local copies, waits for them, and re-layouts  16.1 us (2%)
  between operations  14.2 us (2%)
  other arithmetic  13.7 us (2%)
  loops' own time  11.3 us (2%)
  starting transfers between devices  7.56 us (1%)
    psum x4, waiting for transfers between devices, local(): lax.psum(jnp.dot(image, projector, precision=highest), ('row', 'col'))  530 us
    all_gather x1, waiting for transfers between devices, local(): lax.all_gather(jnp.dot(right_side, projector, precision=highest), ('row',...  57.3 us
    dot_general x12, matrix products, add_slot(): jnp.einsum('rbi,boi->rbo', picked, slot_tiles, preferred_element_type=jnp...  15.7 us
  transfers between devices with their start and end apart: 13, of which 9 were waited for; matrix products, arithmetic and copies ran while one was open for 2% of the time, Pallas kernels for 0%

profile of v1, /device:TPU:1, one launch (start us, length us, event | category | flops | bytes accessed | tf_op | source)
XLA Modules:
  0.0 701.3 jit_solution(8788361380959986782)
XLA Ops:
  7.9 4.2 fusion.73
  13.7 57.3 %all-gather.3.cloned.1.call-done = f32[512,1024]{1,0:T(8,128)} async-done(((f32[16,1024]{1,0:T(8,128)}), f32[512,1024]{1,0:T(8,128)}) %all-gather.3.cloned.1.call-update) | async-done | bytes 2097168 | tf_op jit(solution)/shard_map/all_gather | solution.py:78
  71.0 1.7 reduce_sum.65
  74.9 4.6 copy.86
  80.1 8.4 %while.40 = (s32[]{:T(128)}, f32[16,4,256]{2,0,1:T(8,128)S(1)}, s32[]{:T(128)}, bf16[4,8,256,256]{3,2,0,1:T(8,128)(2,1)}, s32[4,8]{0,1:T(8,128)S(1)}, /*index=5*...) while((s32[]{:T(128)}, f32[16,4,256]{2,0,1:T(8,128)S(1)}, ...), condition=%wide.region_5.7_spmd, body=%wide.region_4.6_spmd.sunk | while | flops 8438813 | bytes 758035 | solution.py:102
  88.6 3.2 fusion.54
  91.9 131.7 %all-reduce.5.cloned.1.call-done = f32[16,1024]{1,0:T(8,128)} async-done(((f32[16,1024]{1,0:T(8,128)}), f32[16,1024]{1,0:T(8,128)}) %all-reduce.5.cloned.1.call-update) | async-done | bytes 65552 | tf_op jit(solution)/shard_map/psum | solution.py:106
  226.7 1.7 collective-permute-start.2
  230.1 1.6 collective-permute-done.2
  231.7 8.4 %while.41 = (s32[]{:T(128)}, f32[16,4,256]{2,0,1:T(8,128)S(1)}, s32[]{:T(128)}, bf16[4,8,256,256]{3,2,0,1:T(8,128)(2,1)}, s32[4,8]{0,1:T(8,128)S(1)}, /*index=5*...) while((s32[]{:T(128)}, f32[16,4,256]{2,0,1:T(8,128)S(1)}, ...), condition=%wide.region_9.11_spmd, body=%wide.region_8.10_spmd.sunk | while | flops 8438813 | bytes 758035 | solution.py:102
  240.1 3.1 fusion.52
  243.6 132.5 %all-reduce.7.cloned.1.call-done = f32[16,1024]{1,0:T(8,128)} async-done(((f32[16,1024]{1,0:T(8,128)}), f32[16,1024]{1,0:T(8,128)}) %all-reduce.7.cloned.1.call-update) | async-done | bytes 65552 | tf_op jit(solution)/shard_map/psum | solution.py:106
  376.1 2.0 fusion.98
  381.6 1.7 collective-permute-start.4
  384.9 1.5 collective-permute-done.4
  386.5 8.4 %while.42 = (s32[]{:T(128)}, f32[16,4,256]{2,0,1:T(8,128)S(1)}, s32[]{:T(128)}, bf16[4,8,256,256]{3,2,0,1:T(8,128)(2,1)}, s32[4,8]{0,1:T(8,128)S(1)}, /*index=5*...) while((s32[]{:T(128)}, f32[16,4,256]{2,0,1:T(8,128)S(1)}, ...), condition=%wide.region_13.15_spmd, body=%wide.region_12.14_spmd.sunk | while | flops 8438813 | bytes 758035 | solution.py:102
  394.9 3.1 fusion.50
  398.3 132.7 %all-reduce.9.cloned.1.call-done = f32[16,1024]{1,0:T(8,128)} async-done(((f32[16,1024]{1,0:T(8,128)}), f32[16,1024]{1,0:T(8,128)}) %all-reduce.9.cloned.1.call-update) | async-done | bytes 65552 | tf_op jit(solution)/shard_map/psum | solution.py:106
  531.0 2.0 fusion.78
  536.5 1.7 collective-permute-start.6
  541.4 8.6 %while.43 = (s32[]{:T(128)}, f32[16,4,256]{2,0,1:T(8,128)S(1)}, s32[]{:T(128)}, bf16[4,8,256,256]{3,2,0,1:T(8,128)(2,1)}, s32[4,8]{0,1:T(8,128)S(1)}, /*index=5*...) while((s32[]{:T(128)}, f32[16,4,256]{2,0,1:T(8,128)S(1)}, ...), condition=%wide.region_17.19_spmd, body=%wide.region_16.18_spmd.sunk | while | flops 8438813 | bytes 758035 | solution.py:102
  550.1 3.1 fusion.48
  553.4 132.7 %all-reduce.11.cloned.1.call-done = f32[16,1024]{1,0:T(8,128)} async-done(((f32[16,1024]{1,0:T(8,128)}), f32[16,1024]{1,0:T(8,128)}) %all-reduce.11.cloned.1.call-update) | async-done | bytes 65552 | tf_op jit(solution)/shard_map/psum | solution.py:106
  686.1 2.1 fusion.90
  (185 shorter events, 51.5 us)
Async XLA Ops:
  7.2 65.7 %copy-start = (f32[16,1024]{1,0:T(8,128)S(1)}, f32[16,1024]{1,0:T(8,128)}, u32[]{:S(2)}) copy-start(f32[16,1024]{1,0:T(8,128)} %param.23) | copy-start | bytes 196612
  7.2 67.5 %copy-start.2 = (s32[4]{0:T(128)S(1)}, s32[4]{0:T(128)}, u32[]{:S(2)}) copy-start(s32[4]{0:T(128)} %param.19) | copy-start | bytes 52
  7.2 63.8 %all-gather.3.cloned.1.call-start = ((), (), s32[]{:S(2)}) async-start(), calls=%async_computation.4 | async-start | bytes 2162688 | tf_op jit(solution)/shard_map/all_gather | solution.py:78
  12.2 211.4 %all-reduce.5.cloned.1.call-start = ((), (), s32[]{:S(2)}) async-start(), calls=%async_computation | async-start | bytes 131072 | tf_op jit(solution)/shard_map/psum | solution.py:106
  72.9 7.2 %collective-permute-start.1 = (bf16[16,1024]{1,0:T(8,128)(2,1)S(1)}, bf16[16,1024]{1,0:T(8,128)(2,1)S(1)}, u32[]{:S(2)}, u32[]{:S(2)}) collective-permute-start(bf16[16,1024]{1,0:T(8,128)(2,1)S(1)} %get-tuple-element.405), channel_id=1, source_target_pairs={{1,0},{2,1},{3,2},{4,3},{5,4},{6,5},{7,6},{8,7},{9,8},{10,9},{11,1... | collective-permute-start | bytes 98312 | tf_op jit(solution)/shard_map/ppermute | solution.py:22
  73.2 6.8 collective-permute-start
  79.4 9.1 %copy-start.1 = (f32[1024]{0:T(1024)S(1)}, f32[1024]{0:T(1024)}, u32[]{:S(2)}) copy-start(f32[1024]{0:T(1024)} %param.20) | copy-start | bytes 12292
  79.4 9.1 %copy-start.3 = (s32[1024]{0:T(1024)S(1)}, s32[1024]{0:T(1024)}, u32[]{:S(2)}) copy-start(s32[1024]{0:T(1024)} %param.21) | copy-start | bytes 12292
  91.7 284.4 %all-reduce.7.cloned.1.call-start = ((), (), s32[]{:S(2)}) async-start(), calls=%async_computation.1 | async-start | bytes 131072 | tf_op jit(solution)/shard_map/psum | solution.py:106
  226.7 3.4 collective-permute-start.3
  226.7 4.9 collective-permute-start.2
  243.3 287.7 %all-reduce.9.cloned.1.call-start = ((), (), s32[]{:S(2)}) async-start(), calls=%async_computation.2 | async-start | bytes 131072 | tf_op jit(solution)/shard_map/psum | solution.py:106
  381.5 3.4 collective-permute-start.5
  381.6 4.9 collective-permute-start.4
  398.1 288.0 %all-reduce.11.cloned.1.call-start = ((), (), s32[]{:S(2)}) async-start(), calls=%async_computation.3 | async-start | bytes 131072 | tf_op jit(solution)/shard_map/psum | solution.py:106
  536.4 3.5 collective-permute-start.7
  536.5 4.9 collective-permute-start.6
Sparse Core Ops, SparseCore 0:
  12.3 58.6 all-gather.2
  91.9 131.7 all-reduce.4
  243.4 132.6 all-reduce.6
  398.2 132.6 all-reduce.8
  553.4 132.6 all-reduce.10
